TPU v7x, 32 devices: a 4x4x1 block of a 4x4x8 slice. The times are simulated.
32 devices in a mesh: part: 1 (over z), data: 4 (over y), model: 8 (over x, core).
Axes of the slice: x: 4, y: 4, z: 1, core: 2. Of those that a mesh axis runs over, the one named last changes fastest.
The devices are a block of a 4x4x8 slice.
Arguments:
- x: bfloat16 [2, 64, 512, 1024], P(None, ('part', 'data'), 'model')
- lengths: int32 [2, 64], P(None, ('part', 'data'))
- norm_gain: bfloat16 [2, 1024], P(None, 'data')
- w_in: bfloat16 [2, 1024, 9216], P(None, 'data', 'model')
- w_kv: bfloat16 [2, 1024, 128], P(None, 'data')
- w_out: bfloat16 [2, 5120, 1024], P(None, 'model', 'data')
Outputs:
- output: bfloat16 [2, 64, 512, 1024], P(None, ('part', 'data'), 'model')
All inputs are finite; a program needn't handle non-finite values.
Results may differ from a plain program's by a relative error of at most 0.013324.
Values are sent between devices in bfloat16 or wider.
A program may use at most 768 MiB of HBM per device.

v0:
```python
import math
import jax
import jax.numpy as jnp
from jax import lax
from jax.sharding import PartitionSpec as P, NamedSharding

NORM_EPS = 1e-6
NEG_BIG = -1e30


def layer_norm(x_act, gain_vec):
    x_f32 = x_act.astype(jnp.float32)
    centered = x_f32 - jnp.mean(x_f32, axis=-1, keepdims=True)
    variance = jnp.mean(centered * centered, axis=-1, keepdims=True)
    return (centered * lax.rsqrt(variance + NORM_EPS) * gain_vec.astype(jnp.float32)).astype(jnp.bfloat16)


def attention(q_heads, k_all, v_all, seq_lens, q_offset):
    q_len = q_heads.shape[1]
    k_len = k_all.shape[1]
    head_dim = k_all.shape[2]
    scores = jnp.einsum("bqhc,bkc->bhqk", q_heads, k_all, preferred_element_type=jnp.float32) * (1.0 / math.sqrt(head_dim))
    q_pos = q_offset + lax.broadcasted_iota(jnp.int32, (q_len, 1), 0)
    k_pos = lax.broadcasted_iota(jnp.int32, (1, k_len), 1)
    allowed = (k_pos <= q_pos)[None, None] & (k_pos[None, None] < seq_lens[:, None, None, None])
    scores = jnp.where(allowed, scores, NEG_BIG)
    attn_probs = jax.nn.softmax(scores, axis=-1).astype(jnp.bfloat16)
    return jnp.einsum("bhqk,bkc->bqhc", attn_probs, v_all, preferred_element_type=jnp.float32).astype(jnp.bfloat16)


def layer_block(x_loc, seq_lens, gain_full, w_in3, w_kv_full, w_out3, n_model):
    n_seqs, t_loc, d_model = x_loc.shape
    head_dim = w_kv_full.shape[1] // 2
    ff_head = (w_in3.shape[2] - head_dim) // 2
    h_loc = layer_norm(x_loc, gain_full)
    h_all = lax.all_gather(h_loc, "model", axis=1, tiled=True)
    projected = jnp.einsum("btd,dhc->bthc", h_all, w_in3, preferred_element_type=jnp.float32).astype(jnp.bfloat16)
    kv_act = jnp.einsum("btd,dc->btc", h_all, w_kv_full, preferred_element_type=jnp.float32).astype(jnp.bfloat16)
    attn_out = attention(projected[..., :head_dim], kv_act[..., :head_dim], kv_act[..., head_dim:], seq_lens, 0)
    gate_act = projected[..., head_dim:head_dim + ff_head]
    up_act = projected[..., head_dim + ff_head:]
    mlp_out = (jax.nn.silu(gate_act.astype(jnp.float32)) * up_act.astype(jnp.float32)).astype(jnp.bfloat16)
    joined = jnp.concatenate([attn_out, mlp_out], axis=-1)
    group_sum = jnp.einsum("bthc,hcd->btd", joined, w_out3, preferred_element_type=jnp.float32).astype(jnp.bfloat16)
    received = lax.all_to_all(group_sum.reshape(n_seqs, n_model, t_loc, d_model), "model", 1, 1, tiled=True)
    z_sum = jnp.sum(received.astype(jnp.float32), axis=1)
    return (x_loc.astype(jnp.float32) + z_sum).astype(jnp.bfloat16)


def solution(mesh):
    n_model = mesh.shape["model"]
    act_spec = P(None, ("part", "data"), "model", None)

    def local_fn(x_blk, len_blk, gain_blk, w_in_blk, w_kv_blk, w_out_blk):
        head_dim = w_kv_blk.shape[2] // 2
        hidden = [x_blk[micro_idx] for micro_idx in range(x_blk.shape[0])]
        for layer_idx in range(gain_blk.shape[0]):
            gain_full = lax.all_gather(gain_blk[layer_idx], "data", axis=0, tiled=True)
            w_in_loc = lax.all_gather(w_in_blk[layer_idx], "data", axis=0, tiled=True)
            w_kv_full = lax.all_gather(w_kv_blk[layer_idx], "data", axis=0, tiled=True)
            w_out_loc = lax.all_gather(w_out_blk[layer_idx], "data", axis=1, tiled=True)
            d_model, in_loc = w_in_loc.shape
            out_loc = w_out_loc.shape[0]
            ff_loc = in_loc - out_loc
            heads_loc = (out_loc - ff_loc) // head_dim
            w_in3 = w_in_loc.reshape(d_model, heads_loc, in_loc // heads_loc)
            w_out3 = w_out_loc.reshape(heads_loc, out_loc // heads_loc, d_model)
            for micro_idx in range(len(hidden)):
                hidden[micro_idx] = layer_block(hidden[micro_idx], len_blk[micro_idx], gain_full, w_in3, w_kv_full, w_out3, n_model)
        return jnp.stack(hidden)

    return jax.shard_map(
        local_fn,
        mesh=mesh,
        in_specs=(act_spec, P(None, ("part", "data")), P(None, "data"), P(None, "data", "model"), P(None, "data", None), P(None, "model", "data")),
        out_specs=act_spec,
        check_vma=False,
    )
```

profile of v0, /device:TPU:97, one launch (start us, length us, event | category | flops | bytes accessed | tf_op | source)
XLA Modules:
  0.0 1277.6 jit_solution(14350660710399583125)
XLA Ops:
  10.5 10.4 all-gather
  23.8 3.0 fusion.88
  32.1 11.7 all-gather.1
  44.0 7.1 broadcast_and_fusion.1
  54.0 75.7 %all-gather.21.cloned.1.call-done = bf16[16,512,1024]{2,1,0:T(8,128)(2,1)} async-done(((bf16[16,64,1024]{2,1,0:T(8,128)(2,1)}), bf16[16,512,1024]{2,1,0:T(8,128)(2,1)}) %all-gather.21.cloned.1.call-update) | async-done | bytes 16777232 | tf_op jit(solution)/shard_map/all_gather | solution.py:36
  129.7 12.7 convolution_convert_fusion.1
  142.4 41.3 %fusion.58 = bf16[16,512,2,576]{1,3,2,0:T(8,128)(2,1)} fusion(bf16[1024,2,576,1]{0,2,1,3:T(8,128)(2,1)S(1)} %bitcast.266, bf16[16,512,1024]{2,1,0:T(8,128)(2,1)} %all-gather.21.cloned.1.call-done), kind=kOutput, calls=%fused_computation.82 | convolution fusion | flops 19336790016 | bytes 38010880 | tf_op jit(solution)/shard_map/btd,dhc->bthc/dot_general | solution.py:37
  183.7 18.3 %fusion.169 = (f32[16,2,512]{2,1,0:T(2,128)S(1)}, f32[16,2,512,512]{2,3,1,0:T(8,128)}) fusion(pred[16,512,512]{1,2,0:T(8,128)(4,1)} %get-tuple-element.24, bf16[16,512,2,576]{1,3,2,0:T(8,128)(2,1)} %fusion.58, bf16[16,512,128]{1,2,0:T(8,128)(2,1)} %convolution_convert_fusion.1), kind=kOutput, calls=%fused_computation.207 | convolution fusion | flops 1107296768 | bytes 40960000 | tf_op jit(solution)/shard_map/sub | solution.py:27
  201.9 11.5 fusion.41
  213.5 13.8 %convert_bitcast_fusion.3 = bf16[16,512,2,64]{1,3,2,0:T(8,128)(2,1)} fusion(f32[16,2,512,512]{2,3,1,0:T(8,128)} %get-tuple-element.36, f32[16,2,512]{2,1,0:T(2,128)S(1)} %get-tuple-element.35, bf16[16,512,128]{1,2,0:T(8,128)(2,1)S(1)} %copy-done.24), kind=kOutput, calls=%fused_computation.146 | convolution fusion | flops 1091567616 | bytes 36765696 | tf_op jit(solution)/shard_map/bhqk,bkc->bqhc/dot_general | solution.py:28
  227.2 21.1 %bitcast_convert_fusion.1 = bf16[16,512,1024]{2,1,0:T(8,128)(2,1)} fusion(bf16[2,320,1024,1]{2,1,0,3:T(8,128)(2,1)} %bitcast.270, bf16[16,512,2,256]{1,3,2,0:T(8,128)(2,1)} %fusion.41, bf16[16,512,2,64]{1,3,2,0:T(8,128)(2,1)} %convert_bitcast_fusion.3), kind=kOutput, calls=%fused_computation.6 | convolution fusion | flops 10766778368 | bytes 28573696 | tf_op jit(solution)/shard_map/bthc,hcd->btd/dot_general | solution.py:44
  248.4 14.1 %copy.17 = bf16[16,8,64,1024]{3,2,0,1:T(8,128)(2,1)} copy(bf16[16,8,64,1024]{3,2,1,0:T(8,128)(2,1)} %bitcast.262) | data formatting | bytes 33554432 | tf_op jit(solution)/shard_map/reshape | solution.py:45
  262.5 6.3 all-to-all-start.2
  268.8 41.3 %fusion.52 = bf16[16,512,2,576]{1,3,2,0:T(8,128)(2,1)} fusion(bf16[1024,2,576,1]{0,2,1,3:T(8,128)(2,1)S(1)} %bitcast.267, bf16[16,512,1024]{2,1,0:T(8,128)(2,1)} %all-gather.17.cloned.1.call-done), kind=kOutput, calls=%fused_computation.80 | convolution fusion | flops 19336790016 | bytes 38010880 | tf_op jit(solution)/shard_map/btd,dhc->bthc/dot_general | solution.py:37
  310.1 11.3 convolution_convert_fusion.3
  321.4 18.8 %fusion.164 = (f32[16,2,512]{2,1,0:T(2,128)S(1)}, f32[16,2,512,512]{2,3,1,0:T(8,128)}) fusion(pred[16,512,512]{1,2,0:T(8,128)(4,1)} %get-tuple-element.23, bf16[16,512,2,576]{1,3,2,0:T(8,128)(2,1)} %fusion.52, bf16[16,512,128]{1,2,0:T(8,128)(2,1)S(1)} %convolution_convert_fusion.3), kind=kOutput, calls=%fused_computation.206 | convolution fusion | flops 1107296768 | bytes 40960000 | tf_op jit(solution)/shard_map/sub | solution.py:27
  340.3 11.7 fusion.43
  352.0 12.6 convert_bitcast_fusion.5
  364.6 20.3 %bitcast_convert_fusion.3 = bf16[16,512,1024]{2,1,0:T(8,128)(2,1)} fusion(bf16[2,320,1024,1]{2,1,0,3:T(8,128)(2,1)S(1)} %bitcast.271, bf16[16,512,2,256]{1,3,2,0:T(8,128)(2,1)} %fusion.43, bf16[16,512,2,64]{1,3,2,0:T(8,128)(2,1)S(1)} %convert_bitcast_fusion.5), kind=kOutput, calls=%fused_computation.10 | convolution fusion | flops 10766778368 | bytes 28573696 | tf_op jit(solution)/shard_map/bthc,hcd->btd/dot_general | solution.py:44
  384.9 14.0 %copy.13 = bf16[16,8,64,1024]{3,2,0,1:T(8,128)(2,1)} copy(bf16[16,8,64,1024]{3,2,1,0:T(8,128)(2,1)} %bitcast.260) | data formatting | bytes 33554432 | tf_op jit(solution)/shard_map/reshape | solution.py:45
  399.0 53.2 %all-to-all-done.2 = bf16[16,8,64,1024]{3,2,0,1:T(8,128)(2,1)} async-done(((bf16[16,8,64,1024]{3,2,0,1:T(8,128)(2,1)}), bf16[16,8,64,1024]{3,2,0,1:T(8,128)(2,1)}, u32[]{:S(2)}, u32[]{:S(2)}) %all-to-all-start.2) | async-done | bytes 16777248 | tf_op jit(solution)/shard_map/all_to_all | solution.py:45
  452.1 6.7 all-to-all-start
  459.5 8.6 all-gather.4
  468.1 9.2 convert_reduce_fusion.1
  477.3 165.0 %all-to-all-done = bf16[16,8,64,1024]{3,2,0,1:T(8,128)(2,1)} async-done(((bf16[16,8,64,1024]{3,2,0,1:T(8,128)(2,1)}), bf16[16,8,64,1024]{3,2,0,1:T(8,128)(2,1)}, u32[]{:S(2)}, u32[]{:S(2)}) %all-to-all-start) | async-done | bytes 16777248 | tf_op jit(solution)/shard_map/all_to_all | solution.py:45
  642.3 8.9 convert_reduce_fusion.3
  659.3 10.7 all-gather.5
  673.0 67.5 %all-gather.23.cloned.1.call-done = bf16[16,512,1024]{2,1,0:T(8,128)(2,1)} async-done(((bf16[16,64,1024]{2,1,0:T(8,128)(2,1)}), bf16[16,512,1024]{2,1,0:T(8,128)(2,1)}) %all-gather.23.cloned.1.call-update) | async-done | bytes 16777232 | tf_op jit(solution)/shard_map/all_gather | solution.py:36
  740.5 12.7 convolution_convert_fusion
  753.2 41.3 %fusion.61 = bf16[16,512,2,576]{1,3,2,0:T(8,128)(2,1)} fusion(bf16[1024,2,576,1]{0,2,1,3:T(8,128)(2,1)S(1)} %bitcast.264, bf16[16,512,1024]{2,1,0:T(8,128)(2,1)} %all-gather.23.cloned.1.call-done), kind=kOutput, calls=%fused_computation.83 | convolution fusion | flops 19336790016 | bytes 38010880 | tf_op jit(solution)/shard_map/btd,dhc->bthc/dot_general | solution.py:37
  794.5 18.3 %fusion.179 = (f32[16,2,512]{2,1,0:T(2,128)S(1)}, f32[16,2,512,512]{2,3,1,0:T(8,128)}) fusion(pred[16,512,512]{1,2,0:T(8,128)(4,1)} %get-tuple-element.24, bf16[16,512,2,576]{1,3,2,0:T(8,128)(2,1)} %fusion.61, bf16[16,512,128]{1,2,0:T(8,128)(2,1)} %convolution_convert_fusion), kind=kOutput, calls=%fused_computation.209 | convolution fusion | flops 1107296768 | bytes 40960000 | tf_op jit(solution)/shard_map/sub | solution.py:27
  812.8 11.6 fusion.40
  824.3 13.8 %convert_bitcast_fusion.2 = bf16[16,512,2,64]{1,3,2,0:T(8,128)(2,1)} fusion(f32[16,2,512,512]{2,3,1,0:T(8,128)} %get-tuple-element.40, f32[16,2,512]{2,1,0:T(2,128)S(1)} %get-tuple-element.39, bf16[16,512,128]{1,2,0:T(8,128)(2,1)S(1)} %copy-done.22), kind=kOutput, calls=%fused_computation.145 | convolution fusion | flops 1091567616 | bytes 36765696 | tf_op jit(solution)/shard_map/bhqk,bkc->bqhc/dot_general | solution.py:28
  838.1 21.1 %bitcast_convert_fusion = bf16[16,512,1024]{2,1,0:T(8,128)(2,1)} fusion(bf16[2,320,1024,1]{2,1,0,3:T(8,128)(2,1)} %bitcast.272, bf16[16,512,2,256]{1,3,2,0:T(8,128)(2,1)} %fusion.40, bf16[16,512,2,64]{1,3,2,0:T(8,128)(2,1)} %convert_bitcast_fusion.2), kind=kOutput, calls=%fused_computation.4 | convolution fusion | flops 10766778368 | bytes 28573696 | tf_op jit(solution)/shard_map/bthc,hcd->btd/dot_general | solution.py:44
  859.2 14.1 %copy.18 = bf16[16,8,64,1024]{3,2,0,1:T(8,128)(2,1)} copy(bf16[16,8,64,1024]{3,2,1,0:T(8,128)(2,1)} %bitcast.263) | data formatting | bytes 33554432 | tf_op jit(solution)/shard_map/reshape | solution.py:45
  873.3 6.5 all-to-all-start.3
  879.8 41.3 %fusion.55 = bf16[16,512,2,576]{1,3,2,0:T(8,128)(2,1)} fusion(bf16[1024,2,576,1]{0,2,1,3:T(8,128)(2,1)S(1)} %bitcast.265, bf16[16,512,1024]{2,1,0:T(8,128)(2,1)} %all-gather.19.cloned.1.call-done), kind=kOutput, calls=%fused_computation.81 | convolution fusion | flops 19336790016 | bytes 38010880 | tf_op jit(solution)/shard_map/btd,dhc->bthc/dot_general | solution.py:37
  921.2 11.3 convolution_convert_fusion.2
  932.5 18.8 %fusion.174 = (f32[16,2,512]{2,1,0:T(2,128)S(1)}, f32[16,2,512,512]{2,3,1,0:T(8,128)}) fusion(pred[16,512,512]{1,2,0:T(8,128)(4,1)} %get-tuple-element.23, bf16[16,512,2,576]{1,3,2,0:T(8,128)(2,1)} %fusion.55, bf16[16,512,128]{1,2,0:T(8,128)(2,1)S(1)} %convolution_convert_fusion.2), kind=kOutput, calls=%fused_computation.208 | convolution fusion | flops 1107296768 | bytes 40960000 | tf_op jit(solution)/shard_map/sub | solution.py:27
  951.3 11.4 fusion.42
  962.8 12.6 convert_bitcast_fusion.4
  975.4 20.3 %bitcast_convert_fusion.2 = bf16[16,512,1024]{2,1,0:T(8,128)(2,1)} fusion(bf16[2,320,1024,1]{2,1,0,3:T(8,128)(2,1)S(1)} %bitcast.273, bf16[16,512,2,256]{1,3,2,0:T(8,128)(2,1)} %fusion.42, bf16[16,512,2,64]{1,3,2,0:T(8,128)(2,1)S(1)} %convert_bitcast_fusion.4), kind=kOutput, calls=%fused_computation.8 | convolution fusion | flops 10766778368 | bytes 28573696 | tf_op jit(solution)/shard_map/bthc,hcd->btd/dot_general | solution.py:44
  995.7 14.0 %copy.16 = bf16[16,8,64,1024]{3,2,0,1:T(8,128)(2,1)} copy(bf16[16,8,64,1024]{3,2,1,0:T(8,128)(2,1)} %bitcast.261) | data formatting | bytes 33554432 | tf_op jit(solution)/shard_map/reshape | solution.py:45
  1009.7 53.4 %all-to-all-done.3 = bf16[16,8,64,1024]{3,2,0,1:T(8,128)(2,1)} async-done(((bf16[16,8,64,1024]{3,2,0,1:T(8,128)(2,1)}), bf16[16,8,64,1024]{3,2,0,1:T(8,128)(2,1)}, u32[]{:S(2)}, u32[]{:S(2)}) %all-to-all-start.3) | async-done | bytes 16777248 | tf_op jit(solution)/shard_map/all_to_all | solution.py:45
  1063.2 7.1 all-to-all-start.1
  1070.2 9.2 convert_reduce_fusion
  1079.5 174.1 %all-to-all-done.1 = bf16[16,8,64,1024]{3,2,0,1:T(8,128)(2,1)} async-done(((bf16[16,8,64,1024]{3,2,0,1:T(8,128)(2,1)}), bf16[16,8,64,1024]{3,2,0,1:T(8,128)(2,1)}, u32[]{:S(2)}, u32[]{:S(2)}) %all-to-all-start.1) | async-done | bytes 16777248 | tf_op jit(solution)/shard_map/all_to_all | solution.py:45
  1253.6 8.9 convert_reduce_fusion.2
  (100 shorter events, 34.6 us)
Async XLA Ops:
  6.5 44.6 %all-gather.25.cloned.1.call-start = ((), (), s32[]{:S(2)}) async-start(), calls=%async_computation.8 | async-start | bytes 2949120 | tf_op jit(solution)/shard_map/all_gather | solution.py:59
  8.9 120.7 %all-gather.21.cloned.1.call-start = ((), (), s32[]{:S(2)}) async-start(), calls=%async_computation.6 | async-start | bytes 18874368 | tf_op jit(solution)/shard_map/all_gather | solution.py:36
  9.0 17.8 %copy-start = (bf16[2,16,64,1024]{3,2,1,0:T(8,128)(2,1)S(1)}, bf16[2,16,64,1024]{3,2,1,0:T(8,128)(2,1)}, u32[]{:S(2)}) copy-start(bf16[2,16,64,1024]{3,2,1,0:T(8,128)(2,1)} %param.6) | copy-start | bytes 12582916
  23.7 6.0 copy-start.8
  23.8 7.6 copy-start.14
  26.8 17.1 %copy-start.16 = (s32[2,16]{1,0:T(2,128)S(1)}, s32[2,16]{1,0:T(2,128)}, u32[]{:S(2)}) copy-start(s32[2,16]{1,0:T(2,128)} %param.7) | copy-start | bytes 388
  29.7 197.6 %all-gather.27.cloned.1.call-start = ((), (), s32[]{:S(2)}) async-start(), calls=%async_computation.9 | async-start | bytes 1638400 | tf_op jit(solution)/shard_map/all_gather | solution.py:61
  30.7 238.1 %all-gather.17.cloned.1.call-start = ((), (), s32[]{:S(2)}) async-start(), calls=%async_computation.4 | async-start | bytes 18874368 | tf_op jit(solution)/shard_map/all_gather | solution.py:36
  43.8 98.6 %copy-start.9 = (bf16[1,1024,128]{1,2,0:T(8,128)(2,1)}, bf16[1,1024,128]{1,2,0:T(8,128)(2,1)S(1)}, u32[]{:S(2)}) copy-start(bf16[1,1024,128]{1,2,0:T(8,128)(2,1)S(1)} %all-gather.1) | copy-start | bytes 786436
  201.9 11.5 copy-start.24
  262.5 189.6 %all-to-all-start.2 = ((bf16[16,8,64,1024]{3,2,0,1:T(8,128)(2,1)}), bf16[16,8,64,1024]{3,2,0,1:T(8,128)(2,1)}, u32[]{:S(2)}, u32[]{:S(2)}) async-start(bf16[16,8,64,1024]{3,2,0,1:T(8,128)(2,1)} %copy.17), calls=%async_computation.2 | async-start | bytes 33554432 | tf_op jit(solution)/shard_map/all_to_all | solution.py:45
  268.7 41.4 %copy-start.10 = (bf16[1,1024,128]{1,2,0:T(8,128)(2,1)S(1)}, bf16[1,1024,128]{1,2,0:T(8,128)(2,1)}, u32[]{:S(2)}) copy-start(bf16[1,1024,128]{1,2,0:T(8,128)(2,1)} %copy-done.9) | copy-start | bytes 786436
  321.4 18.8 %copy-start.21 = (bf16[16,512,128]{1,2,0:T(8,128)(2,1)}, bf16[16,512,128]{1,2,0:T(8,128)(2,1)S(1)}, u32[]{:S(2)}) copy-start(bf16[16,512,128]{1,2,0:T(8,128)(2,1)S(1)} %convolution_convert_fusion.3) | copy-start | bytes 6291460
  352.0 12.6 copy-start.19
  398.9 60.5 %copy-start.15 = (bf16[1,256]{1,0:T(2,128)(2,1)S(1)}, bf16[1,256]{1,0:T(2,128)(2,1)}, u32[]{:S(2)}) copy-start(bf16[1,256]{1,0:T(2,128)(2,1)} %get-tuple-element.31) | copy-start | bytes 1540
  452.1 190.2 %all-to-all-start = ((bf16[16,8,64,1024]{3,2,0,1:T(8,128)(2,1)}), bf16[16,8,64,1024]{3,2,0,1:T(8,128)(2,1)}, u32[]{:S(2)}, u32[]{:S(2)}) async-start(bf16[16,8,64,1024]{3,2,0,1:T(8,128)(2,1)} %copy.13), calls=%async_computation | async-start | bytes 33554432 | tf_op jit(solution)/shard_map/all_to_all | solution.py:45
  458.8 211.2 %all-gather.29.cloned.1.call-start = ((), (), s32[]{:S(2)}) async-start(), calls=%async_computation.10 | async-start | bytes 2949120 | tf_op jit(solution)/shard_map/all_gather | solution.py:59
  459.4 281.1 %all-gather.23.cloned.1.call-start = ((), (), s32[]{:S(2)}) async-start(), calls=%async_computation.7 | async-start | bytes 18874368 | tf_op jit(solution)/shard_map/all_gather | solution.py:36
  642.3 8.9 copy-start.1
  642.3 8.9 copy-start.3
  651.2 2.1 copy-start.5
  653.3 5.8 copy-start.13
  657.5 180.6 %all-gather.31.cloned.1.call-start = ((), (), s32[]{:S(2)}) async-start(), calls=%async_computation.11 | async-start | bytes 1638400 | tf_op jit(solution)/shard_map/all_gather | solution.py:61
  658.4 221.5 %all-gather.19.cloned.1.call-start = ((), (), s32[]{:S(2)}) async-start(), calls=%async_computation.5 | async-start | bytes 18874368 | tf_op jit(solution)/shard_map/all_gather | solution.py:36
  670.0 83.3 %copy-start.11 = (bf16[1,1024,128]{1,2,0:T(8,128)(2,1)}, bf16[1,1024,128]{1,2,0:T(8,128)(2,1)S(1)}, u32[]{:S(2)}) copy-start(bf16[1,1024,128]{1,2,0:T(8,128)(2,1)S(1)} %all-gather.5) | copy-start | bytes 786436
  812.8 11.6 copy-start.22
  873.3 189.8 %all-to-all-start.3 = ((bf16[16,8,64,1024]{3,2,0,1:T(8,128)(2,1)}), bf16[16,8,64,1024]{3,2,0,1:T(8,128)(2,1)}, u32[]{:S(2)}, u32[]{:S(2)}) async-start(bf16[16,8,64,1024]{3,2,0,1:T(8,128)(2,1)} %copy.18), calls=%async_computation.3 | async-start | bytes 33554432 | tf_op jit(solution)/shard_map/all_to_all | solution.py:45
  879.8 41.4 %copy-start.12 = (bf16[1,1024,128]{1,2,0:T(8,128)(2,1)S(1)}, bf16[1,1024,128]{1,2,0:T(8,128)(2,1)}, u32[]{:S(2)}) copy-start(bf16[1,1024,128]{1,2,0:T(8,128)(2,1)} %copy-done.11) | copy-start | bytes 786436
  932.5 18.8 %copy-start.23 = (bf16[16,512,128]{1,2,0:T(8,128)(2,1)}, bf16[16,512,128]{1,2,0:T(8,128)(2,1)S(1)}, u32[]{:S(2)}) copy-start(bf16[16,512,128]{1,2,0:T(8,128)(2,1)S(1)} %convolution_convert_fusion.2) | copy-start | bytes 6291460
  962.8 12.6 copy-start.20
  1063.2 190.4 %all-to-all-start.1 = ((bf16[16,8,64,1024]{3,2,0,1:T(8,128)(2,1)}), bf16[16,8,64,1024]{3,2,0,1:T(8,128)(2,1)}, u32[]{:S(2)}, u32[]{:S(2)}) async-start(bf16[16,8,64,1024]{3,2,0,1:T(8,128)(2,1)} %copy.16), calls=%async_computation.1 | async-start | bytes 33554432 | tf_op jit(solution)/shard_map/all_to_all | solution.py:45
  1253.6 9.0 copy-start.2
  1253.6 9.0 copy-start.4
  1253.6 9.6 copy-start.6
  1253.6 10.7 copy-start.7
  1253.6 11.9 copy-start.17
  1268.5 2.0 copy-start.18
Sparse Core Ops, SparseCore 0:
  9.1 35.5 all-gather.24
  46.2 83.3 all-gather.20
  131.2 23.1 all-gather.26
  155.9 85.2 all-gather.16
  460.9 31.0 all-gather.28
  657.7 82.7 all-gather.22
  742.0 23.1 all-gather.30
  766.9 85.2 all-gather.18
where the time goes:
time: 1280 us
  waiting for transfers between devices  592 us (46%)
  matrix products  423 us (33%)
  other arithmetic  107 us (8%)
  local copies, waits for them, and re-layouts  73.6 us (6%)
  blocking collectives  41.4 us (3%)
  starting transfers between devices  26.9 us (2%)
  between operations  14.2 us (1%)
    all_to_all x4, waiting for transfers between devices, layer_block(): lax.all_to_all(group_sum.reshape(n_seqs, n_model, t_loc, d_model), 'model...  446 us
    dot_general x4, matrix products, layer_block(): jnp.einsum('btd,dhc->bthc', h_all, w_in3, preferred_element_type=jnp.floa...  165 us
    all_gather x4, waiting for transfers between devices, layer_block(): h_all = lax.all_gather(h_loc, 'model', axis=1, tiled=True)  143 us
    dot_general x4, matrix products, layer_block(): jnp.einsum('bthc,hcd->btd', joined, w_out3, preferred_element_type=jnp.fl...  82.8 us
    sub x4, matrix products, attention(): attn_probs = jax.nn.softmax(scores, axis=-1).astype(jnp.bfloat16)  74.2 us
    reshape x4, local copies, waits for them, and re-layouts, layer_block(): group_sum.reshape(n_seqs, n_model, t_loc, d_model)  56.3 us
    dot_general x4, matrix products, attention(): jnp.einsum('bhqk,bkc->bqhc', attn_probs, v_all, preferred_element_type=jn...  52.7 us
    dot_general x4, matrix products, layer_block(): jnp.einsum('btd,dc->btc', h_all, w_kv_full, preferred_element_type=jnp.fl...  48.1 us
  transfers between devices with their start and end apart: 12, of which 6 were waited for; matrix products, arithmetic and copies ran while one was open for 46% of the time, Pallas kernels for 0%

commit v1 on v0

v1 whole, which is shorter than its diff:
```python
import functools
import math
import jax
import jax.numpy as jnp
from jax import lax
from jax.experimental import pallas as pl
from jax.experimental.pallas import tpu as pltpu
from jax.sharding import PartitionSpec as P

NORM_EPS = 1e-6
NEG_BIG = -1e30
LANES = 128
SEQS_BLOCK = 8
CORES = 2
IN_SPLIT = 80
OUT_SPLIT = 320
BF16 = jnp.bfloat16
F32 = jnp.float32


def silu_mul(g, u):
    return g * (1.0 / (1.0 + jnp.exp(-g))) * u


def kernel_body(cfg, lens, x_hbm, w_in_hbm, w_out_hbm, w_kv_in, gain_in,
                y_hbm, all_in, all_out,
                w_in_buf, w_out_buf, kv_land, w_kv_all, gain_all, x_scr, h_scr, z_scr, t_scr, j_scr,
                rsem, ssem, load_sem, io_sem, own_sem):
    n_layers, n_y, n_x, t_loc, s_len, head_dim, in_loc, out_loc, n_seqs = cfg["dims"]
    copies_sem = cfg["sems"]
    d_model = x_scr.shape[1]
    rows_blk = t_scr.shape[0]
    n_blk = x_scr.shape[0] // rows_blk
    seqs_blk = rows_blk // t_loc
    f_loc = d_model // n_y
    n_units = n_x
    my_y = lax.axis_index("data")
    me = lax.axis_index("model")
    my_x, my_c = lax.div(me, CORES), lax.rem(me, CORES)
    q_off = me * t_loc
    order = [0, n_x - 1, 1] + list(range(2, n_x - 1))

    def col(j):
        return lax.rem(my_x + order[j], n_x)

    def at(dy=0, dx=0, dc=0):
        y = lax.rem(my_y + (dy % n_y), n_y)
        x = lax.rem(my_x + (dx % n_x), n_x)
        c = lax.rem(my_c + dc, CORES)
        return {"data": y, "model": x * CORES + c}

    count = [0]
    rings = []

    class Send:
        def __init__(self, dst, to, arrives, src=None):
            self.k = count[0]
            count[0] += 1
            self.dst, self.to, self.arrives, self.src = dst, to, arrives, src or dst
            rings.append(self)

        def make(self, src, dst):
            return pltpu.make_async_remote_copy(src_ref=src, dst_ref=dst, send_sem=ssem.at[self.k], recv_sem=rsem.at[self.k],
                                                device_id=at(**self.to), device_id_type=pl.DeviceIdType.MESH)

        def start(self):
            self.make(self.src(), self.dst()).start()

        def wait(self):
            self.make(self.arrives(), self.arrives()).wait_recv()

        def wait_sent(self):
            self.make(self.src(), self.dst()).wait_send()

    class Ring:
        def __init__(self, axis, piece, flip, own=None):
            n = n_y if axis == "dy" else n_x
            rank = my_y if axis == "dy" else my_x

            def p(d):
                return lambda: piece(lax.rem(rank + (d % n), n))

            self.up = Send(p(0), {axis: 1}, p(-1), own)
            self.down = Send(p(0), {axis: -1}, p(1), own)
            self.flip = flip
            self.far = Send(p(1), {axis: -1}, p(2)) if flip else Send(p(-1), {axis: 1}, p(-2))
            self.p = p

        def start(self):
            self.up.start()
            self.down.start()

        def forward(self):
            (self.down if self.flip else self.up).wait()
            self.far.start()

        def near(self):
            (self.up if self.flip else self.down).wait()

        def last(self):
            self.far.wait()

        def finish(self):
            self.near()
            self.last()

    shards = []
    for l in range(n_layers):
        kinds = []
        for kind, (own, land, split) in enumerate(((w_in_hbm, all_in, IN_SPLIT), (w_out_hbm, all_out, OUT_SPLIT))):
            rows = own.shape[1]
            odd = (l + kind) % 2 == 1
            lo, hi = pl.ds(0, split), pl.ds(split, rows - split)

            def a1(y, land=land, l=l, lo=lo):
                return land.at[l, my_c, my_x, y, lo]

            def a2(x, land=land, l=l, lo=lo):
                return land.at[l, my_c, x, :, lo]

            def b1(x, land=land, l=l, hi=hi):
                return land.at[l, my_c, x, my_y, hi]

            def b2(y, x, land=land, l=l, hi=hi):
                return land.at[l, my_c, x, y, hi]

            def own_lo(own=own, l=l, lo=lo):
                return own.at[l, lo]

            def own_hi(own=own, l=l, hi=hi):
                return own.at[l, hi]

            s = {
                "A1": Ring("dy", a1, odd, own_lo),
                "B1": Ring("dx", b1, not odd, own_hi),
                "A2": Ring("dx", a2, odd),
                "B2": [Ring("dy", (lambda y, j=j, b2=b2: b2(y, col(j))), (j + l + kind) % 2 == 0, own_hi if j == 0 else None) for j in range(n_x)],
                "D": [Send((lambda j=j, land=land, l=l: land.at[l, my_c, col(j)]), {"dc": 1},
                           (lambda j=j, land=land, l=l: land.at[l, 1 - my_c, col(j)])) for j in range(n_x)],
            }
            kinds.append(s)
        shards.append(kinds)

    kvs = []
    for l in range(n_layers):
        for b in range(n_blk):
            def kv_piece(x, c, l=l, b=b):
                return kv_land.at[l, pl.ds(b * seqs_blk, seqs_blk), pl.ds(pl.multiple_of((x * CORES + c) * t_loc, t_loc), t_loc)]

            ring = Ring("dx", (lambda x, f=kv_piece: f(x, my_c)), b % 2 == 1)
            side = []
            for d in (0, -1, 1, 2):
                def there(d=d, f=kv_piece):
                    return f(lax.rem(my_x + (d % n_x), n_x), my_c)

                def here(d=d, f=kv_piece):
                    return f(lax.rem(my_x + (d % n_x), n_x), 1 - my_c)

                side.append(Send(there, {"dc": 1}, here))
            kvs.append((ring, side))

    small = []
    for d in range(1, n_y):
        for src, dst in ((w_kv_in, w_kv_all), (gain_in, gain_all)):
            small.append(Send((lambda dst=dst: dst.at[:, my_y]), {"dy": d},
                              (lambda dst=dst, d=d: dst.at[:, lax.rem(my_y + n_y - d, n_y)]), (lambda src=src: src)))
    assert count[0] == copies_sem, count[0]

    def blk_rows(b):
        return pl.ds(pl.multiple_of(b * rows_blk, rows_blk), rows_blk)

    def load_in(l, j, slot):
        return [pltpu.make_async_copy(all_in.at[l, c, col(j)], w_in_buf.at[slot, :, :, pl.ds(c * in_loc, in_loc)], load_sem.at[slot, c]) for c in range(CORES)]

    def load_out(l, j, slot):
        return [pltpu.make_async_copy(all_out.at[l, c, col(j)], w_out_buf.at[slot, :, pl.ds(c * out_loc, out_loc)], load_sem.at[slot, 2 + c]) for c in range(CORES)]

    def norm_block(l, b):
        rows = blk_rows(b)
        gain = jnp.concatenate([gain_all[l, d, 0:1, :] for d in range(n_y)], axis=1)
        x_f32 = x_scr[rows, :].astype(F32)
        centered = x_f32 - jnp.mean(x_f32, axis=-1, keepdims=True)
        variance = jnp.mean(centered * centered, axis=-1, keepdims=True)
        h_scr[rows, :] = (centered * lax.rsqrt(variance + NORM_EPS) * gain).astype(BF16)
        kv = jnp.dot(h_scr[rows, :], w_kv_all[l].reshape(d_model, 2 * head_dim), preferred_element_type=F32).astype(BF16)
        kv_land[l, pl.ds(b * seqs_blk, seqs_blk), pl.ds(pl.multiple_of(q_off, t_loc), t_loc), :] = kv.reshape(seqs_blk, t_loc, 2 * head_dim)

    def kv_start(l, b):
        ring, side = kvs[l * n_blk + b]
        ring.start()
        side[0].start()

    def kv_forward(l, b):
        ring, side = kvs[l * n_blk + b]
        ring.forward()
        side[2 if ring.flip else 1].start()

    def kv_finish(l, b):
        ring, side = kvs[l * n_blk + b]
        ring.near()
        side[1 if ring.flip else 2].start()
        ring.last()
        side[3].start()
        for s in side:
            s.wait()

    barrier = pltpu.get_barrier_semaphore()
    peers = [{"dy": d} for d in range(1, n_y)] + [{"dx": 1}, {"dx": -1}, {"dc": 1}]
    for to in peers:
        pl.semaphore_signal(barrier, inc=1, device_id=at(**to), device_id_type=pl.DeviceIdType.MESH)

    x_in = [pltpu.make_async_copy(x_hbm.at[blk_rows(b)], x_scr.at[blk_rows(b)], io_sem.at[b]) for b in range(n_blk)]
    own = []
    for l in range(n_layers):
        own.append((w_in_hbm.at[l], w_in_buf.at[1, l, :, pl.ds(0, in_loc)], all_in.at[l, my_c, my_x, my_y], own_sem.at[l, 0]))
        own.append((w_out_hbm.at[l], w_out_buf.at[1, l, pl.ds(0, out_loc)], all_out.at[l, my_c, my_x, my_y], own_sem.at[l, 1]))
    for cp in x_in:
        cp.start()
    for src, mid, _, sem in own:
        pltpu.make_async_copy(src, mid, sem).start()
    pl.semaphore_wait(barrier, len(peers))
    for s in small:
        s.start()
    (i0, o0), (i1, o1) = shards
    i0["A1"].start()
    i0["B1"].start()
    i0["B2"][0].start()
    w_kv_all[:, my_y] = w_kv_in[...]
    gain_all[:, my_y] = gain_in[...]
    for src, mid, dst, sem in own:
        pltpu.make_async_copy(src, mid, sem).wait()
        pltpu.make_async_copy(mid, dst, sem).start()
    for s in small:
        s.wait()
    for cp in x_in:
        cp.wait()

    def first_norm(b, carry):
        norm_block(0, b)
        return carry

    lax.fori_loop(0, n_blk, first_norm, 0)
    for _, mid, dst, sem in own:
        pltpu.make_async_copy(mid, dst, sem).wait()
    for b in range(n_blk):
        kv_start(0, b)
    for ring in (o0["A1"], o0["B1"], o0["B2"][0]):
        ring.start()
    i0["A1"].forward()
    i0["B1"].forward()
    i0["B2"][0].forward()
    i0["A1"].finish()
    i0["A2"].start()
    i0["B2"][0].finish()
    i0["D"][0].start()
    i0["B1"].finish()
    for j in range(1, n_x):
        i0["B2"][j].start()
    i0["D"][0].wait()
    for cp in load_in(0, 0, 0):
        cp.start()

    def clear(b, carry):
        z_scr[blk_rows(b), :] = jnp.zeros((rows_blk, d_model), F32)
        return carry

    lax.fori_loop(0, n_blk, clear, 0)

    top, attn, late = {}, {}, {}

    def put(where, step, *acts):
        where.setdefault(step, []).extend(acts)

    def begin(cps):
        return lambda: [cp.start() for cp in cps()]

    def end(cps):
        return lambda: [cp.wait() for cp in cps()]

    steps_layer = n_units * n_blk

    def fetch(l, j, step, in_first=None):
        slot = (l * n_units + j) % 2
        i, o = shards[l]
        g = l * steps_layer + j * n_blk
        if in_first is None:
            put(late, step, i["D"][j].wait, begin(lambda: load_in(l, j, slot)))
        put(top, g, end(lambda: load_in(l, j, slot)))
        put(late, g if j == 0 and l == 0 else step, o["D"][j].wait, begin(lambda: load_out(l, j, slot)))
        put(late, g, end(lambda: load_out(l, j, slot)))

    for b in range(n_blk):
        put(attn, 0, lambda b=b: kv_forward(0, b))
    for b in range(n_blk):
        put(attn, b, lambda b=b: kv_finish(0, b))
    put(late, 0, o0["A1"].forward, o0["B1"].forward, o0["B2"][0].forward, o0["A1"].finish, o0["A2"].start, o0["B2"][0].finish, o0["D"][0].start)
    fetch(0, 0, 0, in_first=True)
    put(attn, 1, o0["B1"].finish, *[o0["B2"][j].start for j in range(1, n_x)])
    put(top, 2, i0["A2"].forward, i0["B2"][1].forward)
    put(top, 3, i0["B2"][2].forward, i0["B2"][1].finish)
    a2_first, a2_second = ((i0["A2"].down, i0["A2"].up) if i0["A2"].flip else (i0["A2"].up, i0["A2"].down))
    put(top, 3, i0["A2"].near, i0["D"][1].start, i0["B2"][2].finish, i0["D"][2].start)
    put(late, 3, i0["B2"][3].forward, o0["A2"].forward, o0["B2"][1].forward, o0["B2"][2].forward, o0["B2"][1].finish, o0["A2"].near, o0["D"][1].start)
    fetch(0, 1, 3)
    put(attn, 5, o0["B2"][2].finish, o0["D"][2].start, o0["B2"][3].forward)
    put(late, 6, i0["A2"].last, i0["B2"][3].finish, i0["D"][3].start)
    fetch(0, 2, 7)
    put(late, 8, o0["A2"].last, o0["B2"][3].finish, o0["D"][3].start)
    fetch(0, 3, 11)
    put(top, 7, *[r.start for r in (i1["A1"], i1["B1"], i1["B2"][0], o1["A1"], o1["B1"], o1["B2"][0])])
    put(attn, 9, i1["A1"].forward, i1["B1"].forward, i1["B2"][0].forward)
    put(top, 10, o1["A1"].forward, o1["B1"].forward, o1["B2"][0].forward, i1["A1"].finish, i1["A2"].start)
    put(attn, 10, i1["B2"][0].finish, i1["D"][0].start, i1["B1"].finish, *[i1["B2"][j].start for j in range(1, n_x)])
    put(top, 11, o1["A1"].finish, o1["A2"].start, o1["B2"][0].finish, o1["D"][0].start, o1["B1"].finish, *[o1["B2"][j].start for j in range(1, n_x)])
    put(top, 13, i1["A2"].forward, i1["B2"][1].forward, i1["B2"][2].forward)
    put(top, 14, i1["A2"].near, i1["B2"][1].finish, i1["D"][1].start, i1["B2"][2].finish, i1["D"][2].start)
    fetch(1, 0, 15)
    put(top, 15, o1["A2"].forward, i1["B2"][3].forward, o1["B2"][1].forward, o1["B2"][2].forward)
    put(top, 17, o1["A2"].near, o1["B2"][1].finish, o1["D"][1].start, o1["B2"][2].finish, o1["D"][2].start, o1["B2"][3].forward)
    put(top, 18, i1["A2"].last, i1["B2"][3].finish, i1["D"][3].start)
    fetch(1, 1, 19)
    put(top, 20, o1["A2"].last, o1["B2"][3].finish, o1["D"][3].start)
    fetch(1, 2, 23)
    fetch(1, 3, 27)
    for b in range(n_blk):
        put(attn, steps_layer - n_blk + b + 1, lambda b=b: kv_forward(1, b))
        put(attn, steps_layer + b, lambda b=b: kv_finish(1, b))

    def run(where, g):
        for step, acts in sorted(where.items()):
            @pl.when(g == step)
            def _(acts=acts):
                for act in acts:
                    act()

    n_in = w_in_buf.shape[3]
    tiles_in, tiles_out = in_loc // LANES, out_loc // LANES
    low = lax.broadcasted_iota(jnp.int32, (rows_blk, LANES), 1) < head_dim
    low_q = lax.broadcasted_iota(jnp.int32, (t_loc, LANES), 1) < head_dim
    row_pos = q_off + lax.broadcasted_iota(jnp.int32, (t_loc, 1), 0)
    key_pos = lax.broadcasted_iota(jnp.int32, (t_loc, s_len), 1)
    scale = 1.0 / math.sqrt(head_dim)

    def step(g, carry):
        l = lax.div(g, steps_layer)
        u = lax.rem(lax.div(g, n_blk), n_units)
        b = lax.rem(g, n_blk)
        slot = lax.rem(lax.div(g, n_blk), 2)
        rows = blk_rows(b)
        run(top, g)
        h_blk = h_scr[rows, :]
        for c in range(0, n_in, 256):
            w = w_in_buf[slot, :, :, c:c + 256].reshape(d_model, 256)
            t_scr[:, c:c + 256] = jnp.dot(h_blk, w, preferred_element_type=F32).astype(BF16)

        def tile(i):
            return t_scr[:, i * LANES:(i + 1) * LANES].astype(F32)

        for c in range(CORES):
            ti, tj = c * tiles_in, c * tiles_out
            for gate, up, out in ((1, 3, 1), (5, 7, 3), (6, 8, 4)):
                j_scr[:, (tj + out) * LANES:(tj + out + 1) * LANES] = silu_mul(tile(ti + gate), tile(ti + up)).astype(BF16)
            t2 = tile(ti + 2)
            mixed = silu_mul(jnp.where(low, t2, tile(ti)), jnp.where(low, tile(ti + 4), t2)).astype(BF16)
            j_scr[:, tj * LANES:(tj + 1) * LANES] = mixed
            j_scr[:, (tj + 2) * LANES:(tj + 3) * LANES] = mixed
        run(attn, g)

        def one_seq(i, c_seq):
            r = pl.ds(pl.multiple_of(i * t_loc, t_loc), t_loc)
            heads = []
            for c in range(CORES):
                ti = c * tiles_in
                q0 = t_scr[r, ti * LANES:(ti + 1) * LANES].astype(F32)
                q1 = pltpu.roll(t_scr[r, (ti + 4) * LANES:(ti + 5) * LANES].astype(F32), head_dim, 1)
                heads += [jnp.where(low_q, q, 0.0).astype(BF16) for q in (q0, q1)]
            seq = b * seqs_blk + i
            kv = kv_land[l, seq]
            scores = lax.dot_general(jnp.concatenate(heads, axis=0), kv, (((1,), (1,)), ((), ())), preferred_element_type=F32)
            allowed = key_pos < jnp.minimum(row_pos + 1, lens[seq])
            probs = []
            for k in range(len(heads)):
                s = jnp.where(allowed, scores[k * t_loc:(k + 1) * t_loc] * scale, NEG_BIG)
                e = jnp.exp(s - jnp.max(s, axis=-1, keepdims=True))
                probs.append((e * (1.0 / jnp.sum(e, axis=-1, keepdims=True))).astype(BF16))
            o = jnp.dot(jnp.concatenate(probs, axis=0), kv, preferred_element_type=F32)
            for c in range(CORES):
                tj = c * tiles_out
                c0, c2 = slice(tj * LANES, (tj + 1) * LANES), slice((tj + 2) * LANES, (tj + 3) * LANES)
                o_a = pltpu.roll(o[2 * c * t_loc:(2 * c + 1) * t_loc], head_dim, 1)
                o_b = o[(2 * c + 1) * t_loc:(2 * c + 2) * t_loc]
                j_scr[r, c0] = jnp.where(low_q, o_a, j_scr[r, c0].astype(F32)).astype(BF16)
                j_scr[r, c2] = jnp.where(low_q, j_scr[r, c2].astype(F32), o_b).astype(BF16)
            return c_seq

        lax.fori_loop(0, seqs_blk, one_seq, 0)
        run(late, g)
        for n in range(n_y):
            cols = slice(n * f_loc, (n + 1) * f_loc)
            total = z_scr[rows, cols]
            for c in range(CORES):
                part = slice(c * out_loc, (c + 1) * out_loc)
                z_j = jnp.dot(j_scr[:, part], w_out_buf[slot, n, part, :], preferred_element_type=F32)
                total = total + z_j.astype(BF16).astype(F32)
            z_scr[rows, cols] = total

        @pl.when(u == n_units - 1)
        def _():
            x_scr[rows, :] = (x_scr[rows, :].astype(F32) + z_scr[rows, :]).astype(BF16)
            z_scr[rows, :] = jnp.zeros((rows_blk, d_model), F32)

            @pl.when(l < n_layers - 1)
            def _():
                norm_block(1, b)

        for k in range(n_blk):
            @pl.when(g == steps_layer - n_blk + k)
            def _(k=k):
                kv_start(1, k)

            @pl.when(g == n_layers * steps_layer - n_blk + k)
            def _(k=k):
                pltpu.make_async_copy(x_scr.at[blk_rows(k)], y_hbm.at[blk_rows(k)], io_sem.at[k]).start()
        return carry

    lax.fori_loop(0, n_layers * steps_layer, step, 0)
    for s in rings:
        s.wait_sent()
    for b in range(n_blk):
        pltpu.make_async_copy(x_scr.at[blk_rows(b)], y_hbm.at[blk_rows(b)], io_sem.at[b]).wait()


def count_copies(n_layers, n_x, n_y, n_blk):
    per_kind = 3 * (3 + n_x) + n_x
    return n_layers * 2 * per_kind + n_layers * n_blk * 7 + 2 * (n_y - 1)


def run_layers(mesh, x_act, lens, w_in, w_out, w_kv, gain, t_loc):
    n_tok, d_model = x_act.shape
    n_layers, f_loc, in_loc = w_in.shape
    out_loc = w_out.shape[1]
    n_y, n_model = mesh.shape["data"], mesh.shape["model"]
    n_x = n_model // CORES
    head_dim = w_kv.shape[2] // 2
    n_seqs = n_tok // t_loc
    s_len = t_loc * n_model
    rows_blk = SEQS_BLOCK * t_loc
    n_blk = n_tok // rows_blk
    n_sem = count_copies(n_layers, n_x, n_y, n_blk)
    cfg = {"dims": (n_layers, n_y, n_x, t_loc, s_len, head_dim, in_loc, out_loc, n_seqs), "sems": n_sem}
    vmem = pl.BlockSpec(memory_space=pltpu.VMEM)
    hbm = pl.BlockSpec(memory_space=pl.ANY)
    gain8 = jnp.broadcast_to(gain.astype(F32)[:, None, :], (n_layers, 8, f_loc))
    return pl.pallas_call(
        functools.partial(kernel_body, cfg),
        out_shape=(
            jax.ShapeDtypeStruct((n_tok, d_model), BF16),
            jax.ShapeDtypeStruct((n_layers, CORES, n_x, n_y, f_loc, in_loc), BF16),
            jax.ShapeDtypeStruct((n_layers, CORES, n_x, n_y, out_loc, f_loc), BF16),
        ),
        in_specs=[pl.BlockSpec(memory_space=pltpu.SMEM), hbm, hbm, hbm, vmem, vmem],
        out_specs=(hbm, hbm, hbm),
        scratch_shapes=[
            pltpu.VMEM((2, n_y, f_loc, CORES * in_loc), BF16),
            pltpu.VMEM((2, n_y, CORES * out_loc, f_loc), BF16),
            pltpu.VMEM((n_layers, n_seqs, s_len, 2 * head_dim), BF16),
            pltpu.VMEM((n_layers, n_y, f_loc, 2 * head_dim), BF16),
            pltpu.VMEM((n_layers, n_y, 8, f_loc), F32),
            pltpu.VMEM((n_tok, d_model), BF16),
            pltpu.VMEM((n_tok, d_model), BF16),
            pltpu.VMEM((n_tok, d_model), F32),
            pltpu.VMEM((rows_blk, CORES * in_loc), BF16),
            pltpu.VMEM((rows_blk, CORES * out_loc), BF16),
            pltpu.SemaphoreType.DMA((n_sem,)),
            pltpu.SemaphoreType.DMA((n_sem,)),
            pltpu.SemaphoreType.DMA((2, 4)),
            pltpu.SemaphoreType.DMA((n_blk,)),
            pltpu.SemaphoreType.DMA((n_layers, 2)),
        ],
        compiler_params=pltpu.CompilerParams(collective_id=0, has_side_effects=True, vmem_limit_bytes=67043328 - 1024 * 1024),
        name="layers",
    )(lens, x_act, w_in, w_out, w_kv, gain8)[0]


def solution(mesh):
    act_spec = P(None, ("part", "data"), "model", None)

    def local_fn(x_blk, len_blk, gain_blk, w_in_blk, w_kv_blk, w_out_blk):
        n_micro, n_seqs, t_loc, d_model = x_blk.shape
        x_act = x_blk.reshape(n_micro * n_seqs * t_loc, d_model)
        y = run_layers(mesh, x_act, len_blk.reshape(-1), w_in_blk, w_out_blk, w_kv_blk, gain_blk, t_loc)
        return y.reshape(x_blk.shape)

    return jax.shard_map(
        local_fn,
        mesh=mesh,
        in_specs=(act_spec, P(None, ("part", "data")), P(None, "data"), P(None, "data", "model"), P(None, "data", None), P(None, "model", "data")),
        out_specs=act_spec,
        check_vma=False,
    )
```

time: 1280 us -> 451 us (0.35)
  waiting for transfers between devices: 592 us -> 0 us
  Pallas kernels: 0 us -> 443 us
  matrix products: 423 us -> 0 us
  other arithmetic: 107 us -> 0 us
  local copies, waits for them, and re-layouts: 73.6 us -> 7.52 us
  blocking collectives: 41.4 us -> 0 us
  starting transfers between devices: 26.9 us -> 0 us
  between operations: 14.2 us -> 0.01 us
    all_to_all x4 -> x0, waiting for transfers between devices: 446 us -> none  [layer_block(): lax.all_to_all(group_sum.reshape(n_seqs, n_model, t_loc, d_model), 'model...]
    pallas_call x0 -> x1, Pallas kernels: none -> 443 us  [run_layers(): pl.pallas_call(functools.partial(kernel_body, cfg), out_shape=(jax.ShapeD...]
    dot_general x16 -> x0, matrix products: 349 us -> none  [the longest x4 165 us: layer_block(): jnp.einsum('btd,dhc->bthc', h_all, w_in3, preferred_element_type=jnp.floa...]
    all_gather x8 -> x0, waiting for transfers between devices: 143 us -> none  [the longest x4 143 us: layer_block(): h_all = lax.all_gather(h_loc, 'model', axis=1, tiled=True)]
    sub x4 -> x0, matrix products: 74.2 us -> none  [attention(): attn_probs = jax.nn.softmax(scores, axis=-1).astype(jnp.bfloat16)]
    reshape x4 -> x1, local copies, waits for them, and re-layouts: 56.3 us -> 1.32 us  [local_fn(): len_blk.reshape(-1)]
    convert_element_type x10 -> x0, other arithmetic: 54.7 us -> none  [the longest x4 46.2 us: layer_block(): (jax.nn.silu(gate_act.astype(jnp.float32)) * up_act.astype(jnp.float32))....]
    reduce_sum x9 -> x0, other arithmetic: 44.6 us -> none  [the longest x4 36.3 us: layer_block(): z_sum = jnp.sum(received.astype(jnp.float32), axis=1)]
  transfers between devices with their start and end apart: 12 -> 0, of which waited for: 6 -> 0; matrix products, arithmetic and copies ran while one was open for 46% -> 0% of each run, Pallas kernels for 0% -> 0%
where the time goes in v1:
time: 451 us
  Pallas kernels  443 us (98%)
  local copies, waits for them, and re-layouts  7.52 us (2%)
    pallas_call x1, Pallas kernels, run_layers(): pl.pallas_call(functools.partial(kernel_body, cfg), out_shape=(jax.ShapeD...  443 us

profile of v1, /device:TPU:97, one launch (start us, length us, event | category | flops | bytes accessed | tf_op | source)
XLA Modules:
  0.0 450.8 jit_solution(8831507707914897981)
XLA Ops:
  0.0 1.3 reshape.10.lens
  1.3 1.3 broadcast_in_dim.2.gain_in
  2.6 443.3 %layers.1 = (bf16[2048,1024]{1,0:T(8,128)(2,1)}, bf16[2,2,4,4,256,1152]{5,4,3,2,1,0:T(8,128)(2,1)}, bf16[2,2,4,4,640,256]{5,4,3,2,1,0:T(8,128)(2,1)}) custom-call(s32[32]{0:T(128)} %reshape.10.lens, bf16[2048,1024]{1,0:T(8,128)(2,1)} %bitcast.2, bf16[2,256,1152]{2,1,0:T(8,128)(2,1)} %w_in_hbm.1, bf16[2,640,256]{2,1,0:T(8,128)(2,1)} %w_out_hbm.1, ...), custom_call_target="tpu_custom_call" | custom-call | tf_op jit(solution)/shard_map/layers/pallas_call | solution.py:454
  445.9 4.9 %copy.8 = bf16[2,16,64,1024]{3,2,1,0:T(8,128)(2,1)} copy(bf16[2,16,64,1024]{3,2,1,0:T(8,128)(2,1)} %bitcast.3) | data formatting | bytes 8388608

commit v2 on v1

v2 whole, which is shorter than its diff:
```python
import functools
import math
import jax
import jax.numpy as jnp
from jax import lax
from jax.experimental import pallas as pl
from jax.experimental.pallas import tpu as pltpu
from jax.sharding import PartitionSpec as P

NORM_EPS = 1e-6
NEG_BIG = -1e30
LANES = 128
SEQS_BLOCK = 8
SOFT_ROWS = 16
CORES = 2
IN_SPLIT = 80
OUT_SPLIT = 256
BF16 = jnp.bfloat16
F32 = jnp.float32
LINK_RATE, SIDE_RATE = 36e3, 300e3
STEP_TIMES = (2.4, 2.3, 1.6)
BACKLOG = 4.0
RING_WAIT, SIDE_WAIT = 3.0, 2.0


def make_actions(n_layers, n_units, n_blk):
    copies, actions = {}, []
    for l in range(n_layers):
        for k in range(2):
            first = (l + k) % 2 == 1
            rings = [(("A1", l, k), "y", "lo", first), (("B1", l, k), "x", "hi", not first), (("A2", l, k), "x", "lo4", first)]
            rings += [(("B2", l, k, j), "y", "hi", (j + l + k) % 2 == 0) for j in range(n_units)]
            for name, axis, size, flip in rings:
                copies[name + ("up",)] = (axis + "+", (size, k))
                copies[name + ("down",)] = (axis + "-", (size, k))
                copies[name + ("far",)] = (axis + ("-" if flip else "+"), (size, k))
            for j in range(n_units):
                copies[("D", l, k, j)] = ("c", ("all", k))

            def near(name, flip):
                return name + ("down" if flip else "up",)

            def pr(j, extra=0):
                return (l * n_units + j) * 10 + 3 * k + extra

            a1, b1, a2 = ("A1", l, k), ("B1", l, k), ("A2", l, k)
            whole = [a1 + (d,) for d in ("up", "down", "far")]
            for d in ("up", "down"):
                actions.append(([a1 + (d,)], [], pr(0)))
                actions.append(([("B2", l, k, 0, d)], [], pr(0)))
                actions.append(([b1 + (d,)], [], pr(1, -4)))
                actions.append(([a2 + (d,)], whole, pr(1 if d == "up" else 2)))
                for j in range(1, n_units):
                    actions.append(([("B2", l, k, j, d)], [b1 + (("up", "down", "far")[j - 1],)], pr(j)))
            for name, _, _, flip in rings:
                j = {"A1": 0, "B1": n_units - 1, "A2": n_units - 1}.get(name[0], name[-1])
                actions.append(([name + ("far",)], [near(name, flip)], pr(j, -1)))
            for j in range(n_units):
                part = whole if j == 0 else [a2 + (("up", "down", "far")[j - 1],)]
                actions.append(([("D", l, k, j)], part + [("B2", l, k, j, d) for d in ("up", "down", "far")], pr(j, -2)))
    for l in range(n_layers):
        for b in range(n_blk):
            name, flip = ("kv", l, b), b % 2 == 1
            p = l * n_units * 10 + 1 - (5 if l else 0)
            copies[name + ("up",)] = ("x+", ("kv", 0))
            copies[name + ("down",)] = ("x-", ("kv", 0))
            copies[name + ("far",)] = ("x-" if flip else "x+", ("kv", 0))
            for i in range(4):
                copies[("kvs", l, b, i)] = ("c", ("kv", 0))
            actions.append(([name + ("far",)], [name + ("down" if flip else "up",)], p))
            for i, d in enumerate(("up", "down", "far")):
                actions.append(([("kvs", l, b, i + 1)], [name + (d,)], p))
    return copies, actions


def make_plan(n_layers, n_units, n_blk, sizes):
    copies, actions = make_actions(n_layers, n_units, n_blk)
    layer = n_units * n_blk
    queue, done, waited, todo = {}, {}, set(), sorted(actions, key=lambda a: a[2])
    owner = {key: a for a in actions for key in a[0]}
    plan, loaded, now = {}, {}, [0.0]

    def start(key, out):
        link, size = copies[key]
        begin = max(now[0], queue.get(link, 0.0))
        queue[link] = begin + sizes[size] / (SIDE_RATE if link == "c" else LINK_RATE)
        done[key] = queue[link] + (SIDE_WAIT if link == "c" else RING_WAIT)
        out.append(("start", key))

    def wait(key, out):
        if key not in waited:
            now[0] = max(now[0], done[key])
            waited.add(key)
            out.append(("wait", key))

    def sweep(out, must=()):
        moved = True
        while moved:
            moved = False
            for act in list(todo):
                keys, needs, _ = act
                if any(n not in done or (n not in waited and done[n] > now[0]) for n in needs):
                    continue
                if not any(k in must for k in keys) and any(queue.get(copies[k][0], 0.0) > now[0] + BACKLOG for k in keys):
                    continue
                for n in needs:
                    wait(n, out)
                for k in keys:
                    start(k, out)
                todo.remove(act)
                moved = True

    def need(keys, out):
        must, stack = set(), list(keys)
        while stack:
            k = stack.pop()
            if k not in must:
                must.add(k)
                if k in owner:
                    stack += owner[k][1]
        while True:
            sweep(out, must)
            left = [k for k in must if k in done and k not in waited]
            if all(k in waited for k in keys):
                return
            wait(min(left, key=lambda k: done[k]), out)

    def load(l, k, j, out):
        if (l, k, j) not in loaded:
            need([("D", l, k, j)], out)
            out.append(("load", l, k, j))
            loaded[(l, k, j)] = now[0] + 2.5

    def whole(l, k, j):
        ring = ("A1", l, k) if j == 0 else None
        keys = [ring + (d,) for d in ("up", "down", "far")] if ring else [("A2", l, k, ("up", "down", "far")[j - 1])]
        return keys + [("B2", l, k, j, d) for d in ("up", "down", "far")] + [("D", l, k, j)]

    def early(at, out):
        for l in range(n_layers):
            for j in range(n_units):
                for k in range(2):
                    u = l * n_units + j
                    if (l, k, j) in loaded or at < (u - 1) * n_blk:
                        continue
                    if all(q in done and done[q] <= now[0] for q in whole(l, k, j)):
                        need(whole(l, k, j), out)
                        load(l, k, j, out)

    now[0] = 3.0
    plan["entry"] = []
    sweep(plan["entry"])
    now[0] = 12.0
    out = plan["begin"] = []
    for b in range(n_blk):
        for key in (("kv", 0, b, "up"), ("kv", 0, b, "down"), ("kvs", 0, b, 0)):
            start(key, out)
    need(whole(0, 0, 0), out)
    load(0, 0, 0, out)
    for g in range(n_layers * layer):
        l, j, b = g // layer, g // n_blk % n_units, g % n_blk
        out = plan["top", g] = []
        sweep(out)
        early(g, out)
        if b == 0:
            need(whole(l, 0, j), out)
            load(l, 0, j, out)
            now[0] = max(now[0], loaded[(l, 0, j)])
            out.append(("loaded", l, 0, j))
        now[0] += STEP_TIMES[0]
        out = plan["attn", g] = []
        sweep(out)
        early(g, out)
        if j == 0:
            need([("kv", l, b, d) for d in ("up", "down", "far")] + [("kvs", l, b, i) for i in range(4)], out)
        now[0] += STEP_TIMES[1]
        out = plan["late", g] = []
        sweep(out)
        early(g, out)
        if b == 0:
            need(whole(l, 1, j), out)
            load(l, 1, j, out)
            now[0] = max(now[0], loaded[(l, 1, j)])
            out.append(("loaded", l, 1, j))
        now[0] += STEP_TIMES[2]
        if j == n_units - 1:
            now[0] += 0.9
            if l + 1 < n_layers:
                out = plan["end", g] = []
                for key in (("kv", l + 1, b, "up"), ("kv", l + 1, b, "down"), ("kvs", l + 1, b, 0)):
                    start(key, out)
    assert not todo and waited == set(copies)
    return list(copies), plan, now[0]


def silu_mul(g, u):
    return g * (1.0 / (1.0 + jnp.exp(-g))) * u


def kernel_body(cfg, lens, x_hbm, w_in_hbm, w_out_hbm, w_kv_in, gain_in,
                y_hbm, all_in, all_out,
                w_in_buf, w_out_buf, kv_land, w_kv_all, gain_all, x_scr, h_scr, z_scr, t_scr, j_scr, s_a, s_b, p_a, p_b,
                rsem, ssem, load_sem, io_sem, own_sem):
    n_layers, n_y, n_x, t_loc, s_len, head_dim, in_loc, out_loc, n_seqs = cfg["dims"]
    keys, plan = cfg["plan"]
    d_model = x_scr.shape[1]
    rows_blk = t_scr.shape[0]
    n_blk = x_scr.shape[0] // rows_blk
    seqs_blk = rows_blk // t_loc
    f_loc = d_model // n_y
    n_units = n_x
    my_y = lax.axis_index("data")
    me = lax.axis_index("model")
    my_x, my_c = lax.div(me, CORES), lax.rem(me, CORES)
    q_off = me * t_loc
    order = [0, n_x - 1, 1] + list(range(2, n_x - 1))

    def col(j):
        return lax.rem(my_x + order[j], n_x)

    def at(dy=0, dx=0, dc=0):
        y = lax.rem(my_y + (dy % n_y), n_y)
        x = lax.rem(my_x + (dx % n_x), n_x)
        c = lax.rem(my_c + dc, CORES)
        return {"data": y, "model": x * CORES + c}

    sends = {}

    class Send:
        def __init__(self, key, dst, to, arrives, src=None):
            self.k = len(sends)
            self.dst, self.to, self.arrives, self.src = dst, to, arrives, src or dst
            sends[key] = self

        def make(self, src, dst):
            return pltpu.make_async_remote_copy(src_ref=src, dst_ref=dst, send_sem=ssem.at[self.k], recv_sem=rsem.at[self.k],
                                                device_id=at(**self.to), device_id_type=pl.DeviceIdType.MESH)

        def start(self):
            self.make(self.src(), self.dst()).start()

        def wait(self):
            self.make(self.arrives(), self.arrives()).wait_recv()

        def wait_sent(self):
            self.make(self.src(), self.dst()).wait_send()

    def ring(key, axis, piece, flip, own=None):
        n = n_y if axis == "dy" else n_x
        rank = my_y if axis == "dy" else my_x

        def p(d):
            return lambda: piece(lax.rem(rank + (d % n), n))

        Send(key + ("up",), p(0), {axis: 1}, p(-1), own)
        Send(key + ("down",), p(0), {axis: -1}, p(1), own)
        if flip:
            Send(key + ("far",), p(1), {axis: -1}, p(2))
        else:
            Send(key + ("far",), p(-1), {axis: 1}, p(-2))

    for l in range(n_layers):
        for k, (own, land, split) in enumerate(((w_in_hbm, all_in, IN_SPLIT), (w_out_hbm, all_out, OUT_SPLIT))):
            odd = (l + k) % 2 == 1
            lo, hi = pl.ds(0, split), pl.ds(split, own.shape[1] - split)

            def a1(y, land=land, l=l, lo=lo):
                return land.at[l, my_c, my_x, y, lo]

            def a2(x, land=land, l=l, lo=lo):
                return land.at[l, my_c, x, :, lo]

            def b1(x, land=land, l=l, hi=hi):
                return land.at[l, my_c, x, my_y, hi]

            def own_lo(own=own, l=l, lo=lo):
                return own.at[l, lo]

            def own_hi(own=own, l=l, hi=hi):
                return own.at[l, hi]

            ring(("A1", l, k), "dy", a1, odd, own_lo)
            ring(("B1", l, k), "dx", b1, not odd, own_hi)
            ring(("A2", l, k), "dx", a2, odd)
            for j in range(n_units):
                def b2(y, land=land, l=l, hi=hi, j=j):
                    return land.at[l, my_c, col(j), y, hi]

                def unit_of(c, land=land, l=l, j=j):
                    return land.at[l, c, col(j)]

                ring(("B2", l, k, j), "dy", b2, (j + l + k) % 2 == 0, own_hi if j == 0 else None)
                Send(("D", l, k, j), (lambda f=unit_of: f(my_c)), {"dc": 1}, (lambda f=unit_of: f(1 - my_c)))

    for l in range(n_layers):
        for b in range(n_blk):
            def kv_piece(x, c, l=l, b=b):
                return kv_land.at[l, pl.ds(b * seqs_blk, seqs_blk), pl.ds(pl.multiple_of((x * CORES + c) * t_loc, t_loc), t_loc)]

            ring(("kv", l, b), "dx", (lambda x, f=kv_piece: f(x, my_c)), b % 2 == 1)
            for i, d in enumerate((0, -1, 1, 2)):
                def side(c, d=d, f=kv_piece):
                    return f(lax.rem(my_x + (d % n_x), n_x), c)

                Send(("kvs", l, b, i), (lambda f=side: f(my_c)), {"dc": 1}, (lambda f=side: f(1 - my_c)))
    assert set(sends) == set(keys)
    small = []
    for d in range(1, n_y):
        for name, src, dst in (("kv", w_kv_in, w_kv_all), ("gain", gain_in, gain_all)):
            small.append(Send((name, d), (lambda dst=dst: dst.at[:, my_y]), {"dy": d},
                              (lambda dst=dst, d=d: dst.at[:, lax.rem(my_y + n_y - d, n_y)]), (lambda src=src: src)))
    small = [sends[k] for k in sends if k not in set(keys)]

    def blk_rows(b):
        return pl.ds(pl.multiple_of(b * rows_blk, rows_blk), rows_blk)

    def load_in(l, j, slot):
        return [pltpu.make_async_copy(all_in.at[l, c, col(j)], w_in_buf.at[slot, :, :, pl.ds(c * in_loc, in_loc)], load_sem.at[slot, c]) for c in range(CORES)]

    def load_out(l, j, slot):
        return [pltpu.make_async_copy(all_out.at[l, c, col(j)], w_out_buf.at[slot, :, pl.ds(c * out_loc, out_loc)], load_sem.at[slot, 2 + c]) for c in range(CORES)]

    def norm_block(l, b):
        rows = blk_rows(b)
        gain = jnp.concatenate([gain_all[l, d, 0:1, :] for d in range(n_y)], axis=1)
        x_f32 = x_scr[rows, :].astype(F32)
        centered = x_f32 - jnp.mean(x_f32, axis=-1, keepdims=True)
        variance = jnp.mean(centered * centered, axis=-1, keepdims=True)
        h_scr[rows, :] = (centered * lax.rsqrt(variance + NORM_EPS) * gain).astype(BF16)
        kv = jnp.dot(h_scr[rows, :], w_kv_all[l].reshape(d_model, 2 * head_dim), preferred_element_type=F32).astype(BF16)
        kv_land[l, pl.ds(b * seqs_blk, seqs_blk), pl.ds(pl.multiple_of(q_off, t_loc), t_loc), :] = kv.reshape(seqs_blk, t_loc, 2 * head_dim)

    def perform(ops):
        for op, *what in ops:
            if op == "start":
                sends[what[0]].start()
            elif op == "wait":
                sends[what[0]].wait()
            else:
                l, k, j = what
                for cp in (load_out if k else load_in)(l, j, (l * n_units + j) % 2):
                    cp.start() if op == "load" else cp.wait()

    barrier = pltpu.get_barrier_semaphore()
    peers = [{"dy": d} for d in range(1, n_y)] + [{"dx": 1}, {"dx": -1}, {"dc": 1}]
    for to in peers:
        pl.semaphore_signal(barrier, inc=1, device_id=at(**to), device_id_type=pl.DeviceIdType.MESH)

    x_in = [pltpu.make_async_copy(x_hbm.at[blk_rows(b)], x_scr.at[blk_rows(b)], io_sem.at[b]) for b in range(n_blk)]
    own = []
    for l in range(n_layers):
        own.append((w_in_hbm.at[l], w_in_buf.at[1, l, :, pl.ds(0, in_loc)], all_in.at[l, my_c, my_x, my_y], own_sem.at[l, 0]))
        own.append((w_out_hbm.at[l], w_out_buf.at[1, l, pl.ds(0, out_loc)], all_out.at[l, my_c, my_x, my_y], own_sem.at[l, 1]))
    for cp in x_in:
        cp.start()
    for src, mid, _, sem in own:
        pltpu.make_async_copy(src, mid, sem).start()
    pl.semaphore_wait(barrier, len(peers))
    for s in small:
        s.start()
    perform(plan["entry"])
    w_kv_all[:, my_y] = w_kv_in[...]
    gain_all[:, my_y] = gain_in[...]
    for src, mid, dst, sem in own:
        pltpu.make_async_copy(src, mid, sem).wait()
        pltpu.make_async_copy(mid, dst, sem).start()
    for s in small:
        s.wait()
    for cp in x_in:
        cp.wait()

    def first_norm(b, carry):
        norm_block(0, b)
        return carry

    lax.fori_loop(0, n_blk, first_norm, 0)
    for _, mid, dst, sem in own:
        pltpu.make_async_copy(mid, dst, sem).wait()
    perform(plan["begin"])

    def clear(b, carry):
        z_scr[blk_rows(b), :] = jnp.zeros((rows_blk, d_model), F32)
        return carry

    lax.fori_loop(0, n_blk, clear, 0)

    steps_layer = n_units * n_blk

    def run(point, g):
        for step in range(n_layers * steps_layer):
            if plan.get((point, step)):
                @pl.when(g == step)
                def _(step=step):
                    perform(plan[point, step])

    n_in = w_in_buf.shape[3]
    tiles_in, tiles_out = in_loc // LANES, out_loc // LANES
    low = lax.broadcasted_iota(jnp.int32, (rows_blk, LANES), 1) < head_dim
    low_q = lax.broadcasted_iota(jnp.int32, (t_loc, LANES), 1) < head_dim
    row_pos = q_off + lax.broadcasted_iota(jnp.int32, (SOFT_ROWS, 1), 0)
    key_pos = lax.broadcasted_iota(jnp.int32, (SOFT_ROWS, s_len), 1)
    scale = 1.0 / math.sqrt(head_dim)
    s_scr, p_scr = (s_a, s_b), (p_a, p_b)

    def step(g, carry):
        l = lax.div(g, steps_layer)
        u = lax.rem(lax.div(g, n_blk), n_units)
        b = lax.rem(g, n_blk)
        slot = lax.rem(lax.div(g, n_blk), 2)
        rows = blk_rows(b)
        run("top", g)
        h_blk = h_scr[rows, :]
        for c in range(0, n_in, 256):
            w = w_in_buf[slot, :, :, c:c + 256].reshape(d_model, 256)
            t_scr[:, c:c + 256] = jnp.dot(h_blk, w, preferred_element_type=F32).astype(BF16)

        def tile(i):
            return t_scr[:, i * LANES:(i + 1) * LANES].astype(F32)

        for c in range(CORES):
            ti, tj = c * tiles_in, c * tiles_out
            for gate, up, out in ((1, 3, 1), (5, 7, 3), (6, 8, 4)):
                j_scr[:, (tj + out) * LANES:(tj + out + 1) * LANES] = silu_mul(tile(ti + gate), tile(ti + up)).astype(BF16)
            t2 = tile(ti + 2)
            mixed = silu_mul(jnp.where(low, t2, tile(ti)), jnp.where(low, tile(ti + 4), t2)).astype(BF16)
            j_scr[:, tj * LANES:(tj + 1) * LANES] = mixed
            j_scr[:, (tj + 2) * LANES:(tj + 3) * LANES] = mixed
        run("attn", g)

        def score_seq(i):
            r = slice(i * t_loc, (i + 1) * t_loc)
            heads = []
            for c in range(CORES):
                ti = c * tiles_in
                q0 = t_scr[r, ti * LANES:(ti + 1) * LANES].astype(F32)
                q1 = pltpu.roll(t_scr[r, (ti + 4) * LANES:(ti + 5) * LANES].astype(F32), head_dim, 1)
                heads += [jnp.where(low_q, q, 0.0).astype(BF16) for q in (q0, q1)]
            kv = kv_land[l, b * seqs_blk + i]
            s_scr[i % 2][...] = lax.dot_general(jnp.concatenate(heads, axis=0), kv, (((1,), (1,)), ((), ())), preferred_element_type=F32)

        def soft_seq(i):
            for r in range(0, t_loc, SOFT_ROWS):
                bound = jnp.minimum(row_pos + (r + 1), lens[b * seqs_blk + i])
                allowed = key_pos < bound
                for k in range(2 * CORES):
                    part = slice(k * t_loc + r, k * t_loc + r + SOFT_ROWS)
                    s = jnp.where(allowed, s_scr[i % 2][part], NEG_BIG)
                    e = jnp.exp2((s - jnp.max(s, axis=-1, keepdims=True)) * (scale * math.log2(math.e)))
                    p_scr[i % 2][part] = (e * (1.0 / jnp.sum(e, axis=-1, keepdims=True))).astype(BF16)

        def value_seq(i):
            r = slice(i * t_loc, (i + 1) * t_loc)
            o = jnp.dot(p_scr[i % 2][...], kv_land[l, b * seqs_blk + i], preferred_element_type=F32)
            for c in range(CORES):
                tj = c * tiles_out
                c0, c2 = slice(tj * LANES, (tj + 1) * LANES), slice((tj + 2) * LANES, (tj + 3) * LANES)
                o_a = pltpu.roll(o[2 * c * t_loc:(2 * c + 1) * t_loc], head_dim, 1)
                o_b = o[(2 * c + 1) * t_loc:(2 * c + 2) * t_loc]
                j_scr[r, c0] = jnp.where(low_q, o_a, j_scr[r, c0].astype(F32)).astype(BF16)
                j_scr[r, c2] = jnp.where(low_q, j_scr[r, c2].astype(F32), o_b).astype(BF16)

        for i in range(seqs_blk + 2):
            if i < seqs_blk:
                score_seq(i)
            if 0 <= i - 2:
                value_seq(i - 2)
            if 0 <= i - 1 < seqs_blk:
                soft_seq(i - 1)
        run("late", g)
        for n in range(n_y):
            cols = slice(n * f_loc, (n + 1) * f_loc)
            total = z_scr[rows, cols]
            for c in range(CORES):
                part = slice(c * out_loc, (c + 1) * out_loc)
                z_j = jnp.dot(j_scr[:, part], w_out_buf[slot, n, part, :], preferred_element_type=F32)
                total = total + z_j.astype(BF16).astype(F32)
            z_scr[rows, cols] = total

        @pl.when(u == n_units - 1)
        def _():
            x_scr[rows, :] = (x_scr[rows, :].astype(F32) + z_scr[rows, :]).astype(BF16)
            z_scr[rows, :] = jnp.zeros((rows_blk, d_model), F32)

            @pl.when(l < n_layers - 1)
            def _():
                norm_block(1, b)

        run("end", g)
        for k in range(n_blk):
            @pl.when(g == n_layers * steps_layer - n_blk + k)
            def _(k=k):
                pltpu.make_async_copy(x_scr.at[blk_rows(k)], y_hbm.at[blk_rows(k)], io_sem.at[k]).start()
        return carry

    lax.fori_loop(0, n_layers * steps_layer, step, 0)
    for s in sends.values():
        s.wait_sent()
    for b in range(n_blk):
        pltpu.make_async_copy(x_scr.at[blk_rows(b)], y_hbm.at[blk_rows(b)], io_sem.at[b]).wait()


def run_layers(mesh, x_act, lens, w_in, w_out, w_kv, gain, t_loc):
    n_tok, d_model = x_act.shape
    n_layers, f_loc, in_loc = w_in.shape
    out_loc = w_out.shape[1]
    n_y, n_model = mesh.shape["data"], mesh.shape["model"]
    n_x = n_model // CORES
    head_dim = w_kv.shape[2] // 2
    n_seqs = n_tok // t_loc
    s_len = t_loc * n_model
    rows_blk = SEQS_BLOCK * t_loc
    n_blk = n_tok // rows_blk
    sizes = {("kv", 0): SEQS_BLOCK * t_loc * 4 * head_dim}
    for k, (n_rows, n_cols, split) in enumerate(((f_loc, in_loc, IN_SPLIT), (out_loc, f_loc, OUT_SPLIT))):
        row = 2 * n_cols
        sizes |= {("lo", k): split * row, ("lo4", k): n_y * split * row, ("hi", k): (n_rows - split) * row, ("all", k): n_y * n_rows * row}
    keys, plan, _ = make_plan(n_layers, n_x, n_blk, sizes)
    n_sem = len(keys) + 2 * (n_y - 1)
    cfg = {"dims": (n_layers, n_y, n_x, t_loc, s_len, head_dim, in_loc, out_loc, n_seqs), "plan": (keys, plan)}
    vmem = pl.BlockSpec(memory_space=pltpu.VMEM)
    hbm = pl.BlockSpec(memory_space=pl.ANY)
    gain8 = jnp.broadcast_to(gain.astype(F32)[:, None, :], (n_layers, 8, f_loc))
    return pl.pallas_call(
        functools.partial(kernel_body, cfg),
        out_shape=(
            jax.ShapeDtypeStruct((n_tok, d_model), BF16),
            jax.ShapeDtypeStruct((n_layers, CORES, n_x, n_y, f_loc, in_loc), BF16),
            jax.ShapeDtypeStruct((n_layers, CORES, n_x, n_y, out_loc, f_loc), BF16),
        ),
        in_specs=[pl.BlockSpec(memory_space=pltpu.SMEM), hbm, hbm, hbm, vmem, vmem],
        out_specs=(hbm, hbm, hbm),
        scratch_shapes=[
            pltpu.VMEM((2, n_y, f_loc, CORES * in_loc), BF16),
            pltpu.VMEM((2, n_y, CORES * out_loc, f_loc), BF16),
            pltpu.VMEM((n_layers, n_seqs, s_len, 2 * head_dim), BF16),
            pltpu.VMEM((n_layers, n_y, f_loc, 2 * head_dim), BF16),
            pltpu.VMEM((n_layers, n_y, 8, f_loc), F32),
            pltpu.VMEM((n_tok, d_model), BF16),
            pltpu.VMEM((n_tok, d_model), BF16),
            pltpu.VMEM((n_tok, d_model), F32),
            pltpu.VMEM((rows_blk, CORES * in_loc), BF16),
            pltpu.VMEM((rows_blk, CORES * out_loc), BF16),
            pltpu.VMEM((2 * CORES * t_loc, s_len), F32),
            pltpu.VMEM((2 * CORES * t_loc, s_len), F32),
            pltpu.VMEM((2 * CORES * t_loc, s_len), BF16),
            pltpu.VMEM((2 * CORES * t_loc, s_len), BF16),
            pltpu.SemaphoreType.DMA((n_sem,)),
            pltpu.SemaphoreType.DMA((n_sem,)),
            pltpu.SemaphoreType.DMA((2, 4)),
            pltpu.SemaphoreType.DMA((n_blk,)),
            pltpu.SemaphoreType.DMA((n_layers, 2)),
        ],
        compiler_params=pltpu.CompilerParams(collective_id=0, has_side_effects=True, vmem_limit_bytes=67043328 - 1024 * 1024),
        name="layers",
    )(lens, x_act, w_in, w_out, w_kv, gain8)[0]


def solution(mesh):
    act_spec = P(None, ("part", "data"), "model", None)

    def local_fn(x_blk, len_blk, gain_blk, w_in_blk, w_kv_blk, w_out_blk):
        n_micro, n_seqs, t_loc, d_model = x_blk.shape
        x_act = x_blk.reshape(n_micro * n_seqs * t_loc, d_model)
        y = run_layers(mesh, x_act, len_blk.reshape(-1), w_in_blk, w_out_blk, w_kv_blk, gain_blk, t_loc)
        return y.reshape(x_blk.shape)

    return jax.shard_map(
        local_fn,
        mesh=mesh,
        in_specs=(act_spec, P(None, ("part", "data")), P(None, "data"), P(None, "data", "model"), P(None, "data", None), P(None, "model", "data")),
        out_specs=act_spec,
        check_vma=False,
    )
```

time: 451 us -> 333 us (0.74)
  Pallas kernels: 443 us -> 323 us
    pallas_call x1, Pallas kernels: 443 us -> 323 us  [run_layers(): pl.pallas_call(functools.partial(kernel_body, cfg), out_shape=(jax.ShapeD...]
where the time goes in v2:
time: 333 us; the launch traced here: 331 us
  Pallas kernels  323 us (97%)
  local copies, waits for them, and re-layouts  7.52 us (2%)
    pallas_call x1, Pallas kernels, run_layers(): pl.pallas_call(functools.partial(kernel_body, cfg), out_shape=(jax.ShapeD...  323 us

profile of v2, /device:TPU:97, one launch (start us, length us, event | category | flops | bytes accessed | tf_op | source)
XLA Modules:
  0.0 330.8 jit_solution(12097427633360682607)
XLA Ops:
  0.0 1.3 reshape.10.lens
  1.3 1.3 broadcast_in_dim.2.gain_in
  2.6 323.3 %layers.1 = (bf16[2048,1024]{1,0:T(8,128)(2,1)}, bf16[2,2,4,4,256,1152]{5,4,3,2,1,0:T(8,128)(2,1)}, bf16[2,2,4,4,640,256]{5,4,3,2,1,0:T(8,128)(2,1)}) custom-call(s32[32]{0:T(128)} %reshape.10.lens, bf16[2048,1024]{1,0:T(8,128)(2,1)} %bitcast.2, bf16[2,256,1152]{2,1,0:T(8,128)(2,1)} %w_in_hbm.1, bf16[2,640,256]{2,1,0:T(8,128)(2,1)} %w_out_hbm.1, ...), custom_call_target="tpu_custom_call" | custom-call | tf_op jit(solution)/shard_map/layers/pallas_call | solution.py:523
  325.9 4.9 %copy.8 = bf16[2,16,64,1024]{3,2,1,0:T(8,128)(2,1)} copy(bf16[2,16,64,1024]{3,2,1,0:T(8,128)(2,1)} %bitcast.3) | data formatting | bytes 8388608
